TPU v7x, 32 devices: a whole 2x2x4 slice. The times are simulated.
32 devices in a mesh: dp: 16 (over z, x, core), ens: 2 (over y).
Axes of the slice: x: 2, y: 2, z: 4, core: 2. Of those that a mesh axis runs over, the one named last changes fastest.
Arguments:
- embeddings: bfloat16 [12288, 1024], P('dp'), may hold values from -6 to 6
- valid_mask: int32 [12288], P('dp'), may hold values 0 or 1
- first_weight: bfloat16 [2, 1024, 4096], P(None, 'dp', 'ens'), may hold values from -0.1875 to 0.1875
- second_weight: bfloat16 [2, 4096, 128], P(None, 'ens'), may hold values from -0.09375 to 0.09375
- thresholds: int32 [2], replicated, may hold values from -256 to 256
Outputs:
- mean_logits: float32 [12288, 128], P('dp')
- kept_share: float32 [2], P('ens')
- agree_share: float32 [2], P('ens')
All inputs are finite; a program needn't handle non-finite values. No bound on the sum of `valid_mask` on one device may be relied on, other than what follows from the above.
Results may differ from a plain program's by a relative error of at most 0.0044.
Values may be sent and summed in bfloat16 or wider, within the bound.
A program may use at most 64 MiB of HBM per device.

v0:
```python
import jax
import jax.numpy as jnp
from jax import lax
from jax.sharding import PartitionSpec as P


def on_device(embeddings, valid_mask, first_weight, second_weight, thresholds):
    member = lax.axis_index("ens")
    own_first = lax.all_to_all(first_weight, "ens", split_axis=0, concat_axis=2, tiled=True)
    own_second = lax.all_to_all(second_weight, "ens", split_axis=0, concat_axis=1, tiled=True)
    full_first = lax.all_gather(own_first[0], "dp", axis=0, tiled=True)
    hidden = jnp.maximum(
        jnp.dot(embeddings, full_first, preferred_element_type=jnp.float32), 0.0
    ).astype(jnp.bfloat16)
    logits_own = jnp.dot(hidden, own_second[0], preferred_element_type=jnp.float32)
    classes = logits_own.shape[1]
    levels = jnp.arange(classes, dtype=jnp.float32)
    grades = (2.0 * levels / (classes - 1) - 1.0) * jnp.sqrt(jnp.float32(3.0 / classes))
    scores = jnp.dot(logits_own, grades, precision=lax.Precision.HIGHEST)
    cutoffs = thresholds.astype(jnp.float32) / 256.0
    own_cutoff = lax.dynamic_index_in_dim(cutoffs, member, 0, keepdims=False)
    validity = valid_mask.astype(jnp.float32)
    kept_soft = validity * jax.nn.sigmoid(4.0 * (scores - own_cutoff))
    kept_total = lax.psum(jnp.sum(kept_soft), "dp")
    mean_logits = lax.psum(logits_own, "ens") / first_weight.shape[0]
    ens_score = jnp.dot(mean_logits, grades, precision=lax.Precision.HIGHEST)
    ens_kept = jax.nn.sigmoid(4.0 * (ens_score - jnp.mean(cutoffs)))
    agree_local = jnp.sum(kept_soft * ens_kept)
    agree_total = lax.psum(agree_local, "dp")
    shard_docs = embeddings.shape[0]
    return (
        mean_logits,
        (kept_total / shard_docs).reshape(1),
        (agree_total / shard_docs).reshape(1),
    )


def solution(mesh):
    return jax.shard_map(
        on_device,
        mesh=mesh,
        in_specs=(P("dp", None), P("dp"), P(None, "dp", "ens"), P(None, "ens", None), P()),
        out_specs=(P("dp", None), P("ens"), P("ens")),
        check_vma=False,
    )
```

profile of v0, /device:TPU:0, one launch (start us, length us, event | category | flops | bytes accessed | tf_op | source)
XLA Modules:
  0.0 184.1 jit_solution(3838105246013471597)
XLA Ops:
  7.2 0.0 copy-start
  7.2 0.0 all-gather.2.cloned.1.call-start
  7.2 13.1 %all_to_all.24 = bf16[2,64,2048]{2,1,0:T(8,128)(2,1)S(1)} all-to-all(bf16[2,64,2048]{2,1,0:T(8,128)(2,1)} %param.7), channel_id=1, replica_groups=mesh['dp'=16,'ens'=2] {'ens'}, dimensions={0} | all-to-all | bytes 1048576 | tf_op jit(solution)/shard_map/all_to_all | solution.py:9
  20.4 0.5 copy.8
  20.9 1.0 copy.9
  21.9 0.0 all-gather.2.cloned.1.call-update
  21.9 16.9 %all_to_all.25 = bf16[2,2048,128]{2,1,0:T(8,128)(2,1)S(1)} all-to-all(bf16[2,2048,128]{2,1,0:T(8,128)(2,1)} %param.8), channel_id=1, replica_groups=mesh['dp'=16,'ens'=2] {'ens'}, dimensions={0} | all-to-all | bytes 2097152 | tf_op jit(solution)/shard_map/all_to_all | solution.py:10
  38.8 58.1 %all-gather.2.cloned.1.call-done = bf16[1024,4096]{1,0:T(8,128)(2,1)} async-done(((bf16[64,4096]{1,0:T(8,128)(2,1)}), bf16[1024,4096]{1,0:T(8,128)(2,1)}) %all-gather.2.cloned.1.call-update) | async-done | bytes 8388624 | tf_op jit(solution)/shard_map/all_gather | solution.py:11
  96.9 0.0 copy-done
  96.9 0.0 copy-start.4
  96.9 0.0 copy-start.3
  96.9 11.8 %fusion = f32[768,128]{1,0:T(8,128)S(1)} fusion(bf16[4096,128]{1,0:T(8,128)(2,1)S(1)} %bitcast.24, bf16[768,1024]{1,0:T(8,128)(2,1)S(1)} %copy-done, bf16[1024,4096]{1,0:T(8,128)(2,1)} %all-gather.2.cloned.1.call-done), kind=kOutput, calls=%fused_computation.1 | convolution fusion | flops 7254048768 | bytes 11403264 | tf_op jit(solution)/shard_map/dot_general | solution.py:15
  108.7 0.0 copy-start.1
  108.7 0.5 convolution_reduce_fusion.1
  109.2 0.0 all-reduce.3.cloned.1.call-start
  109.2 0.2 copy-done.1
  109.5 0.5 all-reduce.3.cloned.1.call-update
  109.9 0.0 copy-done.4
  110.0 0.6 convert_multiply_fusion
  111.2 0.6 dynamic_slice.4
  111.8 25.5 %all-reduce.3.cloned.1.call-done = f32[768,128]{1,0:T(8,128)} async-done(((f32[768,128]{1,0:T(8,128)}), f32[768,128]{1,0:T(8,128)}) %all-reduce.3.cloned.1.call-update) | async-done | bytes 393232 | tf_op jit(solution)/shard_map/psum | solution.py:25
  137.3 1.0 broadcast_multiply_fusion
  138.3 0.0 copy-start.2
  138.3 0.5 convolution_reduce_fusion
  138.8 0.0 copy-done.3
  138.8 1.3 multiply_reduce_fusion
  140.1 33.6 %all-reduce = (f32[]{:T(128)}, f32[]{:T(128)}) all-reduce(f32[]{:T(128)} %get-tuple-element.4, f32[]{:T(128)} %get-tuple-element.3), channel_id=1, replica_groups=mesh['dp'=16,'ens'=2] {'dp'}, use_global_device_ids=true, to_apply=%region_2.3 | all-reduce | flops 2 | bytes 16 | tf_op jit(solution)/shard_map/psum | solution.py:24
  175.0 0.0 copy-done.2
Async XLA Ops:
  7.2 89.7 %copy-start = (bf16[768,1024]{1,0:T(8,128)(2,1)S(1)}, bf16[768,1024]{1,0:T(8,128)(2,1)}, u32[]{:S(2)}) copy-start(bf16[768,1024]{1,0:T(8,128)(2,1)} %param.5) | copy-start | bytes 4718596
  7.2 89.7 %all-gather.2.cloned.1.call-start = ((), (), s32[]{:S(2)}) async-start(), calls=%async_computation.2 | async-start | bytes 8912896 | tf_op jit(solution)/shard_map/all_gather | solution.py:11
  96.9 13.1 %copy-start.4 = (s32[2]{0:T(128)S(1)}, s32[2]{0:T(128)}, u32[]{:S(2)}) copy-start(s32[2]{0:T(128)} %param.9) | copy-start | bytes 28
  96.9 41.9 %copy-start.3 = (s32[768]{0:T(1024)S(1)}, s32[768]{0:T(1024)}, u32[]{:S(2)}) copy-start(s32[768]{0:T(1024)} %param.6) | copy-start | bytes 9220
  108.7 0.8 copy-start.1
  109.2 28.1 %all-reduce.3.cloned.1.call-start = ((), (), s32[]{:S(2)}) async-start(), calls=%async_computation.3 | async-start | bytes 786432 | tf_op jit(solution)/shard_map/psum | solution.py:25
  138.3 36.7 %copy-start.2 = (f32[768,128]{1,0:T(8,128)}, f32[768,128]{1,0:T(8,128)S(1)}, u32[]{:S(2)}) copy-start(f32[768,128]{1,0:T(8,128)S(1)} %broadcast_multiply_fusion) | copy-start | bytes 1179652
Sparse Core Ops, SparseCore 0:
  22.1 74.7 all-gather.1
  112.9 24.3 all-reduce.2
where the time goes:
time: 184 us
  waiting for transfers between devices  84 us (46%)
  blocking collectives  63.6 us (35%)
  between operations  18.2 us (10%)
  matrix products  12.7 us (7%)
  other arithmetic  2.97 us (2%)
  local copies, waits for them, and re-layouts  2.4 us (1%)
    all_gather x1, waiting for transfers between devices, on_device(): full_first = lax.all_gather(own_first[0], 'dp', axis=0, tiled=True)  58.1 us
    psum x1, blocking collectives, on_device(): kept_total = lax.psum(jnp.sum(kept_soft), 'dp')  33.6 us
    psum x1, waiting for transfers between devices, on_device(): mean_logits = lax.psum(logits_own, 'ens') / first_weight.shape[0]  25.5 us
    all_to_all x1, blocking collectives, on_device(): lax.all_to_all(second_weight, 'ens', split_axis=0, concat_axis=1, tiled=T...  16.9 us
    all_to_all x1, blocking collectives, on_device(): lax.all_to_all(first_weight, 'ens', split_axis=0, concat_axis=2, tiled=True)  13.1 us
    dot_general x1, matrix products, on_device(): jnp.dot(hidden, own_second[0], preferred_element_type=jnp.float32)  11.8 us
  transfers between devices with their start and end apart: 2, of which 2 were waited for; matrix products, arithmetic and copies ran while one was open for 1% of the time, Pallas kernels for 0%

commit v1 on v0

--- a/solution.py
+++ b/solution.py
@@ -22,7 +22,7 @@
     validity = valid_mask.astype(jnp.float32)
     kept_soft = validity * jax.nn.sigmoid(4.0 * (scores - own_cutoff))
     kept_total = lax.psum(jnp.sum(kept_soft), "dp")
-    mean_logits = lax.psum(logits_own, "ens") / first_weight.shape[0]
+    mean_logits = jnp.sum(lax.all_gather(logits_own, "ens"), axis=0) / first_weight.shape[0]
     ens_score = jnp.dot(mean_logits, grades, precision=lax.Precision.HIGHEST)
     ens_kept = jax.nn.sigmoid(4.0 * (ens_score - jnp.mean(cutoffs)))
     agree_local = jnp.sum(kept_soft * ens_kept)

time: 184 us -> 165 us (0.90)
  waiting for transfers between devices: 84 us -> 68.9 us
  blocking collectives: 63.6 us -> 56.1 us
  starting transfers between devices: 0.08 us -> 3.63 us
    psum x1 -> x0, waiting for transfers between devices: 25.5 us -> none  [on_device(): mean_logits = lax.psum(logits_own, 'ens') / first_weight.shape[0]]
    all_to_all x1 -> x0, blocking collectives: 16.9 us -> none  [on_device(): lax.all_to_all(second_weight, 'ens', split_axis=0, concat_axis=1, tiled=T...]
    all_gather x0 -> x1, blocking collectives: none -> 11.9 us  [on_device(): lax.all_gather(logits_own, 'ens')]
    all_to_all x0 -> x1, waiting for transfers between devices: none -> 10.8 us  [on_device(): lax.all_to_all(second_weight, 'ens', split_axis=0, concat_axis=1, tiled=T...]
    all_to_all x0 -> x1, starting transfers between devices: none -> 3.59 us  [on_device(): lax.all_to_all(second_weight, 'ens', split_axis=0, concat_axis=1, tiled=T...]
    psum x1, blocking collectives: 33.6 us -> 31 us  [on_device(): kept_total = lax.psum(jnp.sum(kept_soft), 'dp')]
where the time goes in v1:
time: 165 us
  waiting for transfers between devices  68.9 us (42%)
  blocking collectives  56.1 us (34%)
  between operations  18.2 us (11%)
  matrix products  12.9 us (8%)
  starting transfers between devices  3.63 us (2%)
  other arithmetic  2.69 us (2%)
  local copies, waits for them, and re-layouts  2.11 us (1%)
    all_gather x1, waiting for transfers between devices, on_device(): full_first = lax.all_gather(own_first[0], 'dp', axis=0, tiled=True)  58.1 us
    psum x1, blocking collectives, on_device(): kept_total = lax.psum(jnp.sum(kept_soft), 'dp')  31 us
    all_to_all x1, blocking collectives, on_device(): lax.all_to_all(first_weight, 'ens', split_axis=0, concat_axis=2, tiled=True)  13.1 us
    dot_general x1, matrix products, on_device(): jnp.dot(hidden, own_second[0], preferred_element_type=jnp.float32)  12 us
    all_gather x1, blocking collectives, on_device(): lax.all_gather(logits_own, 'ens')  11.9 us
    all_to_all x1, waiting for transfers between devices, on_device(): lax.all_to_all(second_weight, 'ens', split_axis=0, concat_axis=1, tiled=T...  10.8 us
    all_to_all x1, starting transfers between devices, on_device(): lax.all_to_all(second_weight, 'ens', split_axis=0, concat_axis=1, tiled=T...  3.59 us
  transfers between devices with their start and end apart: 2, of which 2 were waited for; matrix products, arithmetic and copies ran while one was open for 1% of the time, Pallas kernels for 0%

profile of v1, /device:TPU:0, one launch (start us, length us, event | category | flops | bytes accessed | tf_op | source)
XLA Modules:
  0.0 164.5 jit_solution(10188686120547166466)
XLA Ops:
  7.2 0.0 copy-start
  7.2 0.0 all-gather.3.cloned.1.call-start
  7.2 13.1 %all_to_all.24 = bf16[2,64,2048]{2,1,0:T(8,128)(2,1)S(1)} all-to-all(bf16[2,64,2048]{2,1,0:T(8,128)(2,1)} %param.7), channel_id=1, replica_groups=mesh['dp'=16,'ens'=2] {'ens'}, dimensions={0} | all-to-all | bytes 1048576 | tf_op jit(solution)/shard_map/all_to_all | solution.py:9
  20.4 0.5 copy.8
  20.9 1.0 copy.9
  21.9 0.0 all-gather.3.cloned.1.call-update
  21.9 3.6 %all-to-all-start.1 = ((bf16[2,2048,128]{2,1,0:T(8,128)(2,1)}), bf16[2,2048,128]{2,1,0:T(8,128)(2,1)S(1)}, u32[]{:S(2)}, u32[]{:S(2)}) async-start(bf16[2,2048,128]{2,1,0:T(8,128)(2,1)} %param.8), calls=%async_computation.1 | async-start | bytes 2097152 | tf_op jit(solution)/shard_map/all_to_all | solution.py:10
  25.5 1.3 convert_multiply_fusion
  27.4 0.6 dynamic_slice.4
  28.0 10.8 %all-to-all-done.1 = bf16[2,2048,128]{2,1,0:T(8,128)(2,1)S(1)} async-done(((bf16[2,2048,128]{2,1,0:T(8,128)(2,1)}), bf16[2,2048,128]{2,1,0:T(8,128)(2,1)S(1)}, u32[]{:S(2)}, u32[]{:S(2)}) %all-to-all-start.1) | async-done | bytes 1048608 | tf_op jit(solution)/shard_map/all_to_all | solution.py:10
  38.8 0.0 copy-start.2
  38.8 58.1 %all-gather.3.cloned.1.call-done = bf16[1024,4096]{1,0:T(8,128)(2,1)} async-done(((bf16[64,4096]{1,0:T(8,128)(2,1)}), bf16[1024,4096]{1,0:T(8,128)(2,1)}) %all-gather.3.cloned.1.call-update) | async-done | bytes 8388624 | tf_op jit(solution)/shard_map/all_gather | solution.py:11
  96.8 0.0 copy-done.2
  96.8 0.0 copy-done
  96.8 0.0 copy-start.3
  96.8 12.0 %fusion = f32[768,128]{1,0:T(8,128)S(1)} fusion(bf16[4096,128]{1,0:T(8,128)(2,1)} %bitcast.26, bf16[768,1024]{1,0:T(8,128)(2,1)S(1)} %copy-done, bf16[1024,4096]{1,0:T(8,128)(2,1)} %all-gather.3.cloned.1.call-done), kind=kOutput, calls=%fused_computation.1 | convolution fusion | flops 7254048768 | bytes 11403264 | tf_op jit(solution)/shard_map/dot_general | solution.py:15
  108.9 0.5 convolution_reduce_fusion.1
  109.3 11.9 %all-gather = f32[1536,128]{1,0:T(8,128)S(1)} all-gather(f32[768,128]{1,0:T(8,128)S(1)} %fusion), channel_id=2, replica_groups=mesh['dp'=16,'ens'=2] {'ens'}, dimensions={0}, use_global_device_ids=true | all-gather | bytes 1179648 | tf_op jit(solution)/shard_map/all_gather | solution.py:25
  121.3 0.1 reduce_sum.36
  121.4 0.0 copy-start.1
  121.4 0.5 convolution_reduce_fusion
  121.8 0.0 copy-done.3
  121.8 1.3 multiply_reduce_fusion
  123.2 31.0 %all-reduce = (f32[]{:T(128)}, f32[]{:T(128)}) all-reduce(f32[]{:T(128)} %get-tuple-element.4, f32[]{:T(128)} %get-tuple-element.3), channel_id=1, replica_groups=mesh['dp'=16,'ens'=2] {'dp'}, use_global_device_ids=true, to_apply=%region_2.3 | all-reduce | flops 2 | bytes 16 | tf_op jit(solution)/shard_map/psum | solution.py:24
  155.4 0.0 copy-done.1
  (1 shorter events, 0.0 us)
Async XLA Ops:
  7.2 89.7 %copy-start = (bf16[768,1024]{1,0:T(8,128)(2,1)S(1)}, bf16[768,1024]{1,0:T(8,128)(2,1)}, u32[]{:S(2)}) copy-start(bf16[768,1024]{1,0:T(8,128)(2,1)} %param.5) | copy-start | bytes 4718596
  7.2 89.7 %all-gather.3.cloned.1.call-start = ((), (), s32[]{:S(2)}) async-start(), calls=%async_computation.2 | async-start | bytes 8912896 | tf_op jit(solution)/shard_map/all_gather | solution.py:11
  21.9 16.9 %all-to-all-start.1 = ((bf16[2,2048,128]{2,1,0:T(8,128)(2,1)}), bf16[2,2048,128]{2,1,0:T(8,128)(2,1)S(1)}, u32[]{:S(2)}, u32[]{:S(2)}) async-start(bf16[2,2048,128]{2,1,0:T(8,128)(2,1)} %param.8), calls=%async_computation.1 | async-start | bytes 2097152 | tf_op jit(solution)/shard_map/all_to_all | solution.py:10
  38.8 58.1 %copy-start.2 = (bf16[2,2048,128]{2,1,0:T(8,128)(2,1)}, bf16[2,2048,128]{2,1,0:T(8,128)(2,1)S(1)}, u32[]{:S(2)}) copy-start(bf16[2,2048,128]{2,1,0:T(8,128)(2,1)S(1)} %all-to-all-done.1) | copy-start | bytes 3145732
  96.8 25.0 %copy-start.3 = (s32[768]{0:T(1024)S(1)}, s32[768]{0:T(1024)}, u32[]{:S(2)}) copy-start(s32[768]{0:T(1024)} %param.6) | copy-start | bytes 9220
  121.4 34.0 %copy-start.1 = (f32[768,128]{1,0:T(8,128)}, f32[768,128]{1,0:T(8,128)S(1)}, u32[]{:S(2)}) copy-start(f32[768,128]{1,0:T(8,128)S(1)} %broadcast_multiply_fusion) | copy-start | bytes 1179652
Sparse Core Ops, SparseCore 0:
  22.0 74.7 all-gather.2

commit v2 on v0

--- a/solution.py
+++ b/solution.py
@@ -6,7 +6,12 @@
 
 def on_device(embeddings, valid_mask, first_weight, second_weight, thresholds):
     member = lax.axis_index("ens")
-    own_first = lax.all_to_all(first_weight, "ens", split_axis=0, concat_axis=2, tiled=True)
+    own_first = jnp.concatenate(
+        lax.all_to_all(
+            jnp.stack(jnp.split(first_weight, lax.axis_size("ens"), axis=0)), "ens", 0, 0
+        ),
+        axis=2,
+    )
     own_second = lax.all_to_all(second_weight, "ens", split_axis=0, concat_axis=1, tiled=True)
     full_first = lax.all_gather(own_first[0], "dp", axis=0, tiled=True)
     hidden = jnp.maximum(

time: 184 us -> 188 us (1.022)
  matrix products: 12.7 us -> 15.8 us
    dot_general x1, matrix products: 11.8 us -> 14.9 us  [on_device(): jnp.dot(hidden, own_second[0], preferred_element_type=jnp.float32)]
where the time goes in v2:
time: 188 us; the launch traced here: 187 us
  waiting for transfers between devices  84.5 us (45%)
  blocking collectives  62 us (33%)
  between operations  18.3 us (10%)
  matrix products  15.8 us (8%)
  local copies, waits for them, and re-layouts  3.57 us (2%)
  other arithmetic  3.02 us (2%)
    all_gather x1, waiting for transfers between devices, on_device(): full_first = lax.all_gather(own_first[0], 'dp', axis=0, tiled=True)  58.5 us
    psum x1, blocking collectives, on_device(): kept_total = lax.psum(jnp.sum(kept_soft), 'dp')  33.6 us
    psum x1, waiting for transfers between devices, on_device(): mean_logits = lax.psum(logits_own, 'ens') / first_weight.shape[0]  25.5 us
    all_to_all x1, blocking collectives, on_device(): lax.all_to_all(second_weight, 'ens', split_axis=0, concat_axis=1, tiled=T...  16.3 us
    dot_general x1, matrix products, on_device(): jnp.dot(hidden, own_second[0], preferred_element_type=jnp.float32)  14.9 us
    all_to_all x1, blocking collectives, on_device(): lax.all_to_all(jnp.stack(jnp.split(first_weight, lax.axis_size('ens'), ax...  12 us
  transfers between devices with their start and end apart: 2, of which 2 were waited for; matrix products, arithmetic and copies ran while one was open for 1% of the time, Pallas kernels for 0%

profile of v2, /device:TPU:0, one launch (start us, length us, event | category | flops | bytes accessed | tf_op | source)
XLA Modules:
  0.0 187.3 jit_solution(3918088244308441516)
XLA Ops:
  7.2 0.0 copy-start
  7.2 0.0 all-gather.2.cloned.1.call-start
  7.2 1.2 slice_bitcast_fusion.1
  8.4 0.1 pad_maximum_fusion
  8.5 12.0 %all_to_all.14 = bf16[2,1,64,2048]{3,2,1,0:T(8,128)(2,1)S(1)} all-to-all(bf16[2,1,64,2048]{3,2,1,0:T(8,128)(2,1)S(1)} %pad_maximum_fusion), channel_id=1, replica_groups=mesh['dp'=16,'ens'=2] {'ens'}, dimensions={0} | all-to-all | bytes 1048576 | tf_op jit(solution)/shard_map/all_to_all | solution.py:10
  20.5 0.5 copy.8
  21.0 1.0 copy.9
  22.1 0.0 all-gather.2.cloned.1.call-update
  22.1 16.3 %all_to_all.15 = bf16[2,2048,128]{2,1,0:T(8,128)(2,1)S(1)} all-to-all(bf16[2,2048,128]{2,1,0:T(8,128)(2,1)} %param.8), channel_id=1, replica_groups=mesh['dp'=16,'ens'=2] {'ens'}, dimensions={0} | all-to-all | bytes 2097152 | tf_op jit(solution)/shard_map/all_to_all | solution.py:15
  38.4 58.5 %all-gather.2.cloned.1.call-done = bf16[1024,4096]{1,0:T(8,128)(2,1)} async-done(((bf16[64,4096]{1,0:T(8,128)(2,1)}), bf16[1024,4096]{1,0:T(8,128)(2,1)}) %all-gather.2.cloned.1.call-update) | async-done | bytes 8388624 | tf_op jit(solution)/shard_map/all_gather | solution.py:16
  96.9 0.0 copy-done
  96.9 0.0 copy-start.4
  96.9 0.0 copy-start.3
  96.9 14.9 %fusion = f32[768,128]{1,0:T(8,128)S(1)} fusion(bf16[4096,128]{1,0:T(8,128)(2,1)S(1)} %bitcast.26, bf16[1024,4096]{1,0:T(8,128)(2,1)} %all-gather.2.cloned.1.call-done, bf16[768,1024]{1,0:T(8,128)(2,1)S(1)} %copy-done), kind=kOutput, calls=%fused_computation.1 | convolution fusion | flops 7254048768 | bytes 11403264 | tf_op jit(solution)/shard_map/dot_general | solution.py:20
  111.8 0.0 copy-start.1
  111.8 0.5 convolution_reduce_fusion.1
  112.3 0.0 all-reduce.3.cloned.1.call-start
  112.3 0.2 copy-done.1
  112.6 0.5 all-reduce.3.cloned.1.call-update
  113.0 0.0 copy-done.4
  113.1 0.6 convert_multiply_fusion
  113.7 0.6 dynamic_slice.4
  114.9 25.5 %all-reduce.3.cloned.1.call-done = f32[768,128]{1,0:T(8,128)} async-done(((f32[768,128]{1,0:T(8,128)}), f32[768,128]{1,0:T(8,128)}) %all-reduce.3.cloned.1.call-update) | async-done | bytes 393232 | tf_op jit(solution)/shard_map/psum | solution.py:30
  140.4 1.0 broadcast_multiply_fusion
  141.4 0.0 copy-start.2
  141.4 0.5 convolution_reduce_fusion
  141.9 0.0 copy-done.3
  141.9 1.3 multiply_reduce_fusion
  143.2 33.6 %all-reduce = (f32[]{:T(128)}, f32[]{:T(128)}) all-reduce(f32[]{:T(128)} %get-tuple-element.4, f32[]{:T(128)} %get-tuple-element.3), channel_id=1, replica_groups=mesh['dp'=16,'ens'=2] {'dp'}, use_global_device_ids=true, to_apply=%region_2.3 | all-reduce | flops 2 | bytes 16 | tf_op jit(solution)/shard_map/psum | solution.py:29
  178.2 0.0 copy-done.2
Async XLA Ops:
  7.2 89.8 %copy-start = (bf16[768,1024]{1,0:T(8,128)(2,1)S(1)}, bf16[768,1024]{1,0:T(8,128)(2,1)}, u32[]{:S(2)}) copy-start(bf16[768,1024]{1,0:T(8,128)(2,1)} %param.5) | copy-start | bytes 4718596
  7.2 89.7 %all-gather.2.cloned.1.call-start = ((), (), s32[]{:S(2)}) async-start(), calls=%async_computation.2 | async-start | bytes 8912896 | tf_op jit(solution)/shard_map/all_gather | solution.py:16
  96.9 16.1 %copy-start.4 = (s32[2]{0:T(128)S(1)}, s32[2]{0:T(128)}, u32[]{:S(2)}) copy-start(s32[2]{0:T(128)} %param.9) | copy-start | bytes 28
  96.9 44.9 %copy-start.3 = (s32[768]{0:T(1024)S(1)}, s32[768]{0:T(1024)}, u32[]{:S(2)}) copy-start(s32[768]{0:T(1024)} %param.6) | copy-start | bytes 9220
  111.8 0.8 copy-start.1
  112.3 28.1 %all-reduce.3.cloned.1.call-start = ((), (), s32[]{:S(2)}) async-start(), calls=%async_computation.3 | async-start | bytes 786432 | tf_op jit(solution)/shard_map/psum | solution.py:30
  141.4 36.8 %copy-start.2 = (f32[768,128]{1,0:T(8,128)}, f32[768,128]{1,0:T(8,128)S(1)}, u32[]{:S(2)}) copy-start(f32[768,128]{1,0:T(8,128)S(1)} %broadcast_multiply_fusion) | copy-start | bytes 1179652
Sparse Core Ops, SparseCore 0:
  22.2 74.6 all-gather.1
  116.0 24.3 all-reduce.2
